TPU v7x, 32 devices: a whole 2x2x4 slice. The times are simulated.
32 devices in a mesh: grp: 2 (over y), ctx: 4 (over z), hd: 4 (over x, core).
Axes of the slice: x: 2, y: 2, z: 4, core: 2. Of those that a mesh axis runs over, the one named last changes fastest.
Arguments:
- query: bfloat16 [1024, 4096], P(('grp', 'ctx'), 'hd'), parts along dimension 0, may hold values from -6 to 6
- keys: bfloat16 [1024, 1024], P(('grp', 'ctx'), 'hd'), parts along dimension 0, may hold values from -6 to 6
- values: bfloat16 [1024, 1024], P(('grp', 'ctx'), 'hd'), parts along dimension 0, may hold values from -6 to 6
- m_x: bfloat16 [1024, 8192], P(('grp', 'ctx'), 'hd'), parts along dimension 0, may hold values from -6 to 6
- m_z: bfloat16 [1024, 8192], P(('grp', 'ctx'), 'hd'), parts along dimension 0, may hold values from -6 to 6
- m_b: bfloat16 [1024, 1024], P(('grp', 'ctx'), 'hd'), parts along dimension 0, may hold values from -6 to 6
- m_c: bfloat16 [1024, 1024], P(('grp', 'ctx'), 'hd'), parts along dimension 0, may hold values from -0.5 to 0.5
- dt_raw: bfloat16 [1024, 128], P(('grp', 'ctx'), 'hd'), parts along dimension 0, may hold values from -5 to 25
- dt_bias: float32 [128], P('hd'), may hold values from -0.5 to 0.5
- a_log: float32 [128], P('hd'), may hold values from -10 to 0
- d_skip: float32 [128], P('hd'), may hold values from 0.5 to 2
- norm_gain: float32 [8192], P('hd'), may hold values from 0.5 to 1.5
Outputs:
- context: bfloat16 [1024, 4096], P(('grp', 'ctx'), 'hd'), parts along dimension 0
- mixed: bfloat16 [1024, 8192], P(('grp', 'ctx'), 'hd'), parts along dimension 0
There are 2 independent parts, one for each index of `grp`. A program takes and returns all parts, laid end to end along the dimension named above; an argument that names none is the same for every part. Nothing has to cross between parts.
All inputs are finite; a program needn't handle non-finite values.
Results may differ from a plain program's by a relative error of at most 0.009.
Values may be sent and summed in bfloat16 or wider, within the bound.
A program may use at most 64 MiB of HBM per device.

v0:
```python
import math

import jax
import jax.numpy as jnp
from jax import lax
from jax.sharding import PartitionSpec as P

HEAD_SIZE = 128
MP = 64
MN = 128


highest = lax.Precision.HIGHEST
norm_eps = 1e-05
masked_score = -1e30


def token_position(row_index, tok_rows, ctx_count):
    device = row_index // tok_rows
    within = row_index - device * tok_rows
    half_rows = tok_rows // 2
    second = within >= half_rows
    block_index = jnp.where(second, 2 * ctx_count - 1 - device, device)
    return block_index * half_rows + within - jnp.where(second, half_rows, 0)


def pick_block(total_rows, limit):
    selected = 1
    for candidate in range(1, min(total_rows, limit) + 1):
        if total_rows % candidate == 0:
            selected = candidate
    return selected


def folded_to_sequence(whole, ctx_count):
    half_rows = whole.shape[0] // (2 * ctx_count)
    blocks = whole.reshape((ctx_count, 2, half_rows) + whole.shape[1:])
    return jnp.concatenate([blocks[:, 0], blocks[::-1, 1]], axis=0).reshape(whole.shape)


def attend(query, keys, values):
    tok_rows = query.shape[0]
    ctx_count = lax.axis_size("ctx")
    kv_local = keys.shape[1] // HEAD_SIZE
    heads_per_group = query.shape[1] // keys.shape[1]
    query_heads = query.reshape(tok_rows, kv_local, heads_per_group, HEAD_SIZE)
    own_rows = lax.axis_index("ctx") * tok_rows + jnp.arange(tok_rows, dtype=jnp.int32)
    query_pos = token_position(own_rows, tok_rows, ctx_count)
    scaling = 1.0 / math.sqrt(HEAD_SIZE)
    start_max = jnp.full((kv_local, heads_per_group, tok_rows), masked_score, jnp.float32)
    start_sum = jnp.zeros((kv_local, heads_per_group, tok_rows), jnp.float32)
    start_acc = jnp.zeros((kv_local, heads_per_group, tok_rows, HEAD_SIZE), jnp.float32)
    start = jnp.int32(0)
    key_piece = lax.all_gather(keys, "ctx", axis=0, tiled=True)
    value_piece = lax.all_gather(values, "ctx", axis=0, tiled=True)
    piece_rows = key_piece.shape[0]
    rows_per_block = pick_block(piece_rows, 1024)

    def one_block(index, running):
        running_max, running_sum, running_acc = running
        offset = index * rows_per_block
        key_block = lax.dynamic_slice_in_dim(key_piece, offset, rows_per_block, 0).reshape(
            rows_per_block, kv_local, HEAD_SIZE
        )
        value_block = lax.dynamic_slice_in_dim(value_piece, offset, rows_per_block, 0).reshape(
            rows_per_block, kv_local, HEAD_SIZE
        )
        key_pos = token_position(
            start + offset + jnp.arange(rows_per_block, dtype=jnp.int32), tok_rows, ctx_count
        )
        visible = key_pos[None, :] <= query_pos[:, None]
        scores = (
            jnp.einsum("qhgd,khd->hgqk", query_heads, key_block, preferred_element_type=jnp.float32)
            * scaling
        )
        scores = jnp.where(visible, scores, masked_score)
        new_max = jnp.maximum(running_max, jnp.max(scores, axis=-1))
        weights = jnp.where(visible, jnp.exp(scores - new_max[..., None]), 0.0)
        factor = jnp.exp(running_max - new_max)
        new_sum = running_sum * factor + jnp.sum(weights, axis=-1)
        update = jnp.einsum(
            "hgqk,khd->hgqd",
            weights.astype(jnp.bfloat16),
            value_block,
            preferred_element_type=jnp.float32,
        )
        return (new_max, new_sum, running_acc * factor[..., None] + update)

    final_max, final_sum, final_acc = lax.fori_loop(
        0, piece_rows // rows_per_block, one_block, (start_max, start_sum, start_acc)
    )
    averaged = final_acc / final_sum[..., None]
    return jnp.transpose(averaged, (2, 0, 1, 3)).reshape(tok_rows, -1).astype(jnp.bfloat16)


def ssd_block(inputs, steps, rates, b_rows, c_rows):
    intersection = jnp.dot(c_rows, b_rows.T, preferred_element_type=jnp.float32)
    inputs = inputs.astype(jnp.float32)
    b_rows = b_rows.astype(jnp.float32)
    sequence_length = inputs.shape[0]
    running = jnp.cumsum(-steps * rates, axis=0)
    lower = jnp.arange(sequence_length)[:, None] >= jnp.arange(sequence_length)[None, :]
    spread = running[:, None, :] - running[None, :, :]
    decay = jnp.exp(jnp.where(lower[:, :, None], spread, -jnp.inf))
    weights = intersection[:, :, None] * decay * steps[None, :, :]
    inner = jnp.einsum("ijh,jhp->ihp", weights, inputs, precision=highest)
    tail_weight = jnp.exp(running[-1][None, :] - running) * steps
    state = jnp.einsum("jh,jhp,jn->hpn", tail_weight, inputs, b_rows, precision=highest)
    return (inner, state, jnp.exp(running[-1]), jnp.exp(running))


def chain_states(earlier, later):
    return (earlier[0] * later[0], earlier[1] * later[0][..., None, None] + later[1])


def ssd_sequence(inputs, steps, rates, b_rows, c_rows):
    sequence_length, head_count, width = inputs.shape
    block_len = math.gcd(sequence_length, 128)
    count = sequence_length // block_len
    c_blocks = c_rows.reshape(count, block_len, -1)
    inner, state, totals, scaled = jax.vmap(ssd_block, in_axes=(0, 0, None, 0, 0))(
        inputs.reshape(count, block_len, head_count, width),
        steps.reshape(count, block_len, head_count),
        rates,
        b_rows.reshape(count, block_len, -1),
        c_blocks,
    )
    running = lax.associative_scan(chain_states, (totals, state))
    entering = jnp.concatenate([jnp.zeros_like(running[1][:1]), running[1][:-1]], axis=0)
    carried = (
        jnp.einsum("cqn,chpn->cqhp", c_blocks.astype(jnp.float32), entering, precision=highest)
        * scaled[..., None]
    )
    return (inner + carried).reshape(sequence_length, head_count, width)


def gated_norm(gated_rows, norm_scale, group_count):
    row_count = gated_rows.shape[0]
    widened = (
        lax.optimization_barrier(gated_rows).astype(jnp.float32).reshape(row_count, group_count, -1)
    )
    power = jnp.mean(widened * widened, axis=-1, keepdims=True)
    return ((widened * lax.rsqrt(power + norm_eps)).reshape(row_count, -1) * norm_scale).astype(
        jnp.bfloat16
    )


def body(query, keys, values, m_x, m_z, m_b, m_c, dt_raw, dt_bias, a_log, d_skip, norm_gain):
    ctx_count = lax.axis_size("ctx")
    context_fold = attend(query, keys, values)
    heads_here = dt_bias.shape[0]
    groups_here = m_b.shape[1] // MN
    per_group = heads_here // groups_here
    rates = jnp.exp(a_log)
    x_cols, z_cols, context_cols = (
        lax.all_to_all(m_x, "ctx", split_axis=1, concat_axis=0, tiled=True),
        lax.all_to_all(m_z, "ctx", split_axis=1, concat_axis=0, tiled=True),
        lax.all_to_all(context_fold, "ctx", split_axis=1, concat_axis=0, tiled=True),
    )
    dt_whole, b_whole, c_whole = (
        lax.all_gather(dt_raw, "ctx", axis=0, tiled=True),
        lax.all_gather(m_b, "ctx", axis=0, tiled=True),
        lax.all_gather(m_c, "ctx", axis=0, tiled=True),
    )
    x_cols = folded_to_sequence(x_cols, ctx_count)
    z_cols = folded_to_sequence(z_cols, ctx_count)
    context_cols = folded_to_sequence(context_cols, ctx_count)
    dt_whole = folded_to_sequence(dt_whole, ctx_count)
    b_whole = folded_to_sequence(b_whole, ctx_count)
    c_whole = folded_to_sequence(c_whole, ctx_count)
    sequence_length = x_cols.shape[0]
    width = x_cols.shape[1]
    sub_width = min(width, MP)
    head_count = width // sub_width
    first_head = lax.axis_index("ctx") * width // MP
    group_index = first_head // per_group
    step_mine = jax.nn.softplus(
        lax.dynamic_slice_in_dim(dt_whole, first_head, head_count, 1).astype(jnp.float32)
        + lax.dynamic_slice_in_dim(dt_bias, first_head, head_count, 0)
    )
    rate_mine = lax.dynamic_slice_in_dim(rates, first_head, head_count, 0)
    skip_mine = lax.dynamic_slice_in_dim(d_skip, first_head, head_count, 0)
    b_mine = lax.dynamic_slice_in_dim(b_whole, group_index * MN, MN, 1)
    c_mine = lax.dynamic_slice_in_dim(c_whole, group_index * MN, MN, 1)
    x_mine = x_cols.reshape(sequence_length, head_count, sub_width)
    outputs = ssd_sequence(x_mine, step_mine, rate_mine, b_mine, c_mine)
    outputs = outputs + skip_mine[None, :, None] * x_mine.astype(jnp.float32)
    gated = (
        outputs.reshape(sequence_length, width) * jax.nn.silu(z_cols.astype(jnp.float32))
    ).astype(jnp.bfloat16)
    gated_rows, context = (
        lax.all_to_all(gated, "ctx", split_axis=0, concat_axis=1, tiled=True),
        lax.all_to_all(context_cols, "ctx", split_axis=0, concat_axis=1, tiled=True),
    )
    mixed = gated_norm(gated_rows, norm_gain, groups_here)
    return (context, mixed)


def solution(mesh):
    in_specs = (
        P(("grp", "ctx"), "hd"),
        P(("grp", "ctx"), "hd"),
        P(("grp", "ctx"), "hd"),
        P(("grp", "ctx"), "hd"),
        P(("grp", "ctx"), "hd"),
        P(("grp", "ctx"), "hd"),
        P(("grp", "ctx"), "hd"),
        P(("grp", "ctx"), "hd"),
        P("hd"),
        P("hd"),
        P("hd"),
        P("hd"),
    )
    out_specs = (P(("grp", "ctx"), "hd"), P(("grp", "ctx"), "hd"))
    return jax.shard_map(body, mesh=mesh, in_specs=in_specs, out_specs=out_specs, check_vma=False)
```

profile of v0, /device:TPU:0, one launch (start us, length us, event | category | flops | bytes accessed | tf_op | source)
XLA Modules:
  0.0 158.5 jit_solution(12240753231804312375)
XLA Ops:
  0.6 15.9 %all_gather.16 = bf16[512,256]{1,0:T(8,128)(2,1)S(1)} all-gather(bf16[128,256]{1,0:T(8,128)(2,1)} %param.14), channel_id=1, replica_groups=mesh['grp'=2,'ctx'=4,'hd'=4] {'ctx'}, dimensions={0}, use_global_device_ids=true | all-gather | bytes 327680 | tf_op jit(solution)/shard_map/all_gather | solution.py:55
  16.5 0.1 copy.70
  16.7 1.0 copy.67
  17.6 13.3 %all_gather.15 = bf16[512,256]{0,1:T(8,128)(2,1)S(1)} all-gather(bf16[128,256]{0,1:T(8,128)(2,1)S(1)} %copy.67), channel_id=1, replica_groups=mesh['grp'=2,'ctx'=4,'hd'=4] {'ctx'}, dimensions={0}, use_global_device_ids=true | all-gather | bytes 327680 | tf_op jit(solution)/shard_map/all_gather | solution.py:54
  30.9 1.1 reshape.189
  32.0 0.1 broadcast_compare_fusion
  32.2 0.5 fusion.8
  32.8 0.5 fusion.9
  33.3 0.7 fusion.17
  34.0 0.9 copy.72
  34.9 4.2 %all-to-all-start = ((bf16[128,4,256]{2,0,1:T(8,128)(2,1)}), bf16[128,4,256]{2,0,1:T(8,128)(2,1)S(1)}, u32[]{:S(2)}, u32[]{:S(2)}) async-start(bf16[128,4,256]{2,0,1:T(8,128)(2,1)} %copy.72), calls=%async_computation | async-start | bytes 524288 | tf_op jit(solution)/shard_map/all_to_all | solution.py:158
  39.0 13.6 %all_gather.19 = bf16[512,32]{0,1:T(8,128)(2,1)S(1)} all-gather(bf16[128,32]{0,1:T(8,128)(2,1)S(1)} %copy-done.10), channel_id=1, replica_groups=mesh['grp'=2,'ctx'=4,'hd'=4] {'ctx'}, dimensions={0}, use_global_device_ids=true | all-gather | bytes 40960 | tf_op jit(solution)/shard_map/all_gather | solution.py:161
  52.7 0.1 reshape.199
  52.8 0.1 fusion.60
  53.1 0.1 reshape.200
  53.2 0.1 dynamic_slice.25
  53.3 0.1 compare_select_fusion
  53.4 0.1 copy.82
  53.5 0.1 dynamic_slice.26
  53.6 14.5 %all_gather.18 = bf16[512,256]{1,0:T(8,128)(2,1)S(1)} all-gather(bf16[128,256]{1,0:T(8,128)(2,1)S(1)} %copy-done.4), channel_id=1, replica_groups=mesh['grp'=2,'ctx'=4,'hd'=4] {'ctx'}, dimensions={0}, use_global_device_ids=true | all-gather | bytes 327680 | tf_op jit(solution)/shard_map/all_gather | solution.py:162
  68.1 14.5 %all_gather.17 = bf16[512,256]{1,0:T(8,128)(2,1)S(1)} all-gather(bf16[128,256]{1,0:T(8,128)(2,1)S(1)} %copy-done.5), channel_id=1, replica_groups=mesh['grp'=2,'ctx'=4,'hd'=4] {'ctx'}, dimensions={0}, use_global_device_ids=true | all-gather | bytes 327680 | tf_op jit(solution)/shard_map/all_gather | solution.py:163
  82.7 0.3 reduce_window_sum.11
  83.0 0.1 fusion.59
  83.1 0.7 copy.85
  83.8 0.7 copy.83
  84.6 1.0 copy.74
  85.6 1.0 copy.90
  86.6 0.1 copy.88
  86.7 0.1 dynamic_slice.27
  86.9 0.7 mul.219
  87.6 3.5 %all-to-all-start.2 = ((bf16[128,4,512]{0,2,1:T(8,128)(2,1)}), bf16[128,4,512]{0,2,1:T(8,128)(2,1)S(1)}, u32[]{:S(2)}, u32[]{:S(2)}) async-start(bf16[128,4,512]{0,2,1:T(8,128)(2,1)} %bitcast.18), calls=%async_computation.2 | async-start | bytes 1048576 | tf_op jit(solution)/shard_map/all_to_all | solution.py:156
  91.1 0.6 iota_compare_fusion
  91.8 0.9 fusion.61
  92.7 11.7 %all-to-all-done.2 = bf16[128,4,512]{0,2,1:T(8,128)(2,1)S(1)} async-done(((bf16[128,4,512]{0,2,1:T(8,128)(2,1)}), bf16[128,4,512]{0,2,1:T(8,128)(2,1)S(1)}, u32[]{:S(2)}, u32[]{:S(2)}) %all-to-all-start.2) | async-done | bytes 524320 | tf_op jit(solution)/shard_map/all_to_all | solution.py:156
  104.4 3.5 %all-to-all-start.3 = ((bf16[128,4,512]{0,2,1:T(8,128)(2,1)}), bf16[128,4,512]{0,2,1:T(8,128)(2,1)S(1)}, u32[]{:S(2)}, u32[]{:S(2)}) async-start(bf16[128,4,512]{0,2,1:T(8,128)(2,1)} %bitcast.46), calls=%async_computation.3 | async-start | bytes 1048576 | tf_op jit(solution)/shard_map/all_to_all | solution.py:157
  107.9 0.7 pad_maximum_fusion.3
  108.6 0.2 copy.75
  108.9 10.5 %all-to-all-done.3 = bf16[128,4,512]{0,2,1:T(8,128)(2,1)S(1)} async-done(((bf16[128,4,512]{0,2,1:T(8,128)(2,1)}), bf16[128,4,512]{0,2,1:T(8,128)(2,1)S(1)}, u32[]{:S(2)}, u32[]{:S(2)}) %all-to-all-start.3) | async-done | bytes 524320 | tf_op jit(solution)/shard_map/all_to_all | solution.py:157
  119.5 4.2 %all-to-all-start.1 = ((bf16[4,128,256]{2,1,0:T(8,128)(2,1)}), bf16[4,128,256]{2,1,0:T(8,128)(2,1)}, u32[]{:S(2)}, u32[]{:S(2)}) async-start(bf16[4,128,256]{2,1,0:T(8,128)(2,1)} %bitcast.15), calls=%async_computation.1 | async-start | bytes 524288 | tf_op jit(solution)/shard_map/all_to_all | solution.py:193
  123.7 0.2 copy.91
  124.0 0.9 pad_maximum_fusion
  124.9 0.5 reshape_reshape_reshape.3
  125.4 0.6 convert_multiply_fusion
  126.1 1.8 %fusion = f32[4,8,64,128]{3,2,1,0:T(8,128)S(1)} fusion(bf16[4,128,128,1]{2,1,3,0:T(8,128)(2,1)S(1)} %bitcast.143, f32[4,128,8,64]{3,2,1,0:T(8,128)S(1)} %convert_multiply_fusion), kind=kOutput, calls=%fused_computation.1 | convolution fusion | flops 402653184 | bytes 2228224 | tf_op jit(solution)/shard_map/vmap(jh,jhp,jn->hpn)/dot_general | solution.py:108
  127.9 0.1 slice_add_fusion
  128.0 0.1 fusion.58
  128.1 0.9 pad_add_fusion
  128.9 0.1 fusion.57
  129.1 0.2 pad.33
  129.3 6.2 %pad.61 = f32[4,8,64,128]{3,2,1,0:T(8,128)S(1)} pad(f32[2,8,64,128]{3,2,1,0:T(8,128)} %pad_add_fusion, f32[]{:T(128)} %constant.92.clone.1), padding=1_0_1x0_0_0x0_0_0x0_0_0 | pad | bytes 1572868
  135.5 0.1 slice_add_fusion.2
  135.6 0.8 copy-done.3
  136.5 2.7 %fusion.11 = f32[4,128,8,64]{1,3,2,0:T(8,128)S(1)} fusion(bf16[4,128,8,64]{3,2,1,0:T(8,128)(2,1)S(1)} %reshape_reshape_reshape.3, f32[4,128,8]{1,2,0:T(8,128)S(1)} %copy-done.6, f32[4,128,8]{1,2,0:T(8,128)S(1)} %copy-done.7, f32[4,128,128]{2,1,0:T(8,128)S(1)} %copy-done.3, pred[128,128]{1,0:T(8,128)(4,1)S(1)} %copy-done.8), kind=kOutput, calls=%fused_computation.14 | convolution fusion | flops 404750336 | bytes 1884160 | tf_op jit(solution)/shard_map/vmap(ijh,jhp->ihp)/dot_general | solution.py:106
  139.2 0.6 fusion.14
  139.8 0.3 copy.89
  140.2 1.2 fusion.36
  141.4 5.0 %all-to-all-start.4 = ((bf16[4,128,512]{2,1,0:T(8,128)(2,1)}), bf16[4,128,512]{2,1,0:T(8,128)(2,1)S(1)}, u32[]{:S(2)}, u32[]{:S(2)}) async-start(bf16[4,128,512]{2,1,0:T(8,128)(2,1)} %fusion.36), calls=%async_computation.4 | async-start | bytes 1048576 | tf_op jit(solution)/shard_map/all_to_all | solution.py:192
  146.4 1.1 copy.73
  147.5 0.9 copy.94
  148.4 8.3 %all-to-all-done.4 = bf16[4,128,512]{2,1,0:T(8,128)(2,1)S(1)} async-done(((bf16[4,128,512]{2,1,0:T(8,128)(2,1)}), bf16[4,128,512]{2,1,0:T(8,128)(2,1)S(1)}, u32[]{:S(2)}, u32[]{:S(2)}) %all-to-all-start.4) | async-done | bytes 524320 | tf_op jit(solution)/shard_map/all_to_all | solution.py:192
  156.7 0.3 copy.93
  156.9 0.2 bitcast_reduce_fusion
  157.1 0.3 fusion.19
  157.5 1.0 copy.95
  (64 shorter events, 0.8 us)
Async XLA Ops:
  33.3 5.7 %copy-start.10 = (bf16[128,32]{0,1:T(8,128)(2,1)S(1)}, bf16[128,32]{0,1:T(8,128)(2,1)}, u32[]{:S(2)}) copy-start(bf16[128,32]{0,1:T(8,128)(2,1)} %param.19) | copy-start | bytes 24580
  34.0 19.2 %copy-start.12 = (f32[32]{0:T(128)S(1)}, f32[32]{0:T(128)}, u32[]{:S(2)}) copy-start(f32[32]{0:T(128)} %param.20) | copy-start | bytes 388
  34.0 19.5 %copy-start.13 = (f32[32]{0:T(128)S(1)}, f32[32]{0:T(128)}, u32[]{:S(2)}) copy-start(f32[32]{0:T(128)} %param.21) | copy-start | bytes 388
  34.0 19.6 %copy-start.4 = (bf16[128,256]{1,0:T(8,128)(2,1)S(1)}, bf16[128,256]{1,0:T(8,128)(2,1)}, u32[]{:S(2)}) copy-start(bf16[128,256]{1,0:T(8,128)(2,1)} %param.17) | copy-start | bytes 196612
  34.0 34.1 %copy-start.5 = (bf16[128,256]{1,0:T(8,128)(2,1)S(1)}, bf16[128,256]{1,0:T(8,128)(2,1)}, u32[]{:S(2)}) copy-start(bf16[128,256]{1,0:T(8,128)(2,1)} %param.18) | copy-start | bytes 196612
  34.9 52.8 %all-to-all-start = ((bf16[128,4,256]{2,0,1:T(8,128)(2,1)}), bf16[128,4,256]{2,0,1:T(8,128)(2,1)S(1)}, u32[]{:S(2)}, u32[]{:S(2)}) async-start(bf16[128,4,256]{2,0,1:T(8,128)(2,1)} %copy.72), calls=%async_computation | async-start | bytes 524288 | tf_op jit(solution)/shard_map/all_to_all | solution.py:158
  68.1 16.5 %copy-start.1 = (bf16[128,2048]{1,0:T(8,128)(2,1)S(1)}, bf16[128,2048]{1,0:T(8,128)(2,1)}, u32[]{:S(2)}) copy-start(bf16[128,2048]{1,0:T(8,128)(2,1)} %param.15) | copy-start | bytes 1572868
  82.7 2.9 %copy-start.2 = (bf16[128,2048]{1,0:T(8,128)(2,1)S(1)}, bf16[128,2048]{1,0:T(8,128)(2,1)}, u32[]{:S(2)}) copy-start(bf16[128,2048]{1,0:T(8,128)(2,1)} %param.16) | copy-start | bytes 1572868
  83.0 3.7 %copy-start.14 = (f32[32]{0:T(128)S(1)}, f32[32]{0:T(128)}, u32[]{:S(2)}) copy-start(f32[32]{0:T(128)} %param.22) | copy-start | bytes 388
  87.6 16.7 %all-to-all-start.2 = ((bf16[128,4,512]{0,2,1:T(8,128)(2,1)}), bf16[128,4,512]{0,2,1:T(8,128)(2,1)S(1)}, u32[]{:S(2)}, u32[]{:S(2)}) async-start(bf16[128,4,512]{0,2,1:T(8,128)(2,1)} %bitcast.18), calls=%async_computation.2 | async-start | bytes 1048576 | tf_op jit(solution)/shard_map/all_to_all | solution.py:156
  104.4 15.1 %all-to-all-start.3 = ((bf16[128,4,512]{0,2,1:T(8,128)(2,1)}), bf16[128,4,512]{0,2,1:T(8,128)(2,1)S(1)}, u32[]{:S(2)}, u32[]{:S(2)}) async-start(bf16[128,4,512]{0,2,1:T(8,128)(2,1)} %bitcast.46), calls=%async_computation.3 | async-start | bytes 1048576 | tf_op jit(solution)/shard_map/all_to_all | solution.py:157
  119.5 21.9 %all-to-all-start.1 = ((bf16[4,128,256]{2,1,0:T(8,128)(2,1)}), bf16[4,128,256]{2,1,0:T(8,128)(2,1)}, u32[]{:S(2)}, u32[]{:S(2)}) async-start(bf16[4,128,256]{2,1,0:T(8,128)(2,1)} %bitcast.15), calls=%async_computation.1 | async-start | bytes 524288 | tf_op jit(solution)/shard_map/all_to_all | solution.py:193
  135.5 0.9 copy-start.3
  135.5 1.0 copy-start.6
  135.5 1.0 copy-start.7
  135.5 0.9 copy-start.8
  139.2 1.0 copy-start
  139.2 1.0 copy-start.11
  141.4 15.7 %copy-start.9 = (f32[2048]{0:T(1024)S(1)}, f32[2048]{0:T(1024)}, u32[]{:S(2)}) copy-start(f32[2048]{0:T(1024)} %param.23) | copy-start | bytes 24580
  141.4 15.3 %all-to-all-start.4 = ((bf16[4,128,512]{2,1,0:T(8,128)(2,1)}), bf16[4,128,512]{2,1,0:T(8,128)(2,1)S(1)}, u32[]{:S(2)}, u32[]{:S(2)}) async-start(bf16[4,128,512]{2,1,0:T(8,128)(2,1)} %fusion.36), calls=%async_computation.4 | async-start | bytes 1048576 | tf_op jit(solution)/shard_map/all_to_all | solution.py:192
where the time goes:
time: 160 us; the launch traced here: 158 us
  blocking collectives  71.8 us (45%)
  waiting for transfers between devices  30.6 us (19%)
  local copies, waits for them, and re-layouts  20.3 us (13%)
  starting transfers between devices  20.3 us (13%)
  matrix products  7.27 us (5%)
  other arithmetic  7.03 us (4%)
    all_gather x1, blocking collectives, attend(): value_piece = lax.all_gather(values, 'ctx', axis=0, tiled=True)  15.9 us
    all_gather x1, blocking collectives, body(): lax.all_gather(m_c, 'ctx', axis=0, tiled=True)  14.5 us
    all_gather x1, blocking collectives, body(): lax.all_gather(m_b, 'ctx', axis=0, tiled=True)  14.5 us
    all_gather x1, blocking collectives, body(): lax.all_gather(dt_raw, 'ctx', axis=0, tiled=True)  13.6 us
    all_gather x1, blocking collectives, attend(): key_piece = lax.all_gather(keys, 'ctx', axis=0, tiled=True)  13.3 us
    unnamed x36, local copies, waits for them, and re-layouts  12 us
    all_to_all x1, waiting for transfers between devices, body(): lax.all_to_all(m_x, 'ctx', split_axis=1, concat_axis=0, tiled=True)  11.7 us
    all_to_all x1, waiting for transfers between devices, body(): lax.all_to_all(m_z, 'ctx', split_axis=1, concat_axis=0, tiled=True)  10.5 us
  transfers between devices with their start and end apart: 5, of which 3 were waited for; matrix products, arithmetic and copies ran while one was open for 17% of the time, Pallas kernels for 0%

commit v1 on v0

v1 whole, which is shorter than its diff:
```python
import functools
import math

import jax
import jax.numpy as jnp
from jax import lax
from jax.experimental import pallas as pl
from jax.experimental.pallas import tpu as pltpu
from jax.sharding import PartitionSpec as P

HEAD_SIZE = 128
MP = 64
MN = 128
NORM_EPS = 1e-05
MASKED = -1e30
HIGHEST = lax.Precision.HIGHEST
F32 = jnp.float32
BF16 = jnp.bfloat16


def dot(a, b, ca=1, cb=0, precision=None):
    return lax.dot_general(
        a, b, (((ca,), (cb,)), ((), ())), preferred_element_type=F32, precision=precision
    )


def kernel(
    n, q_ref, k_ref, v_ref, x_ref, z_ref, b_ref, c_ref, dt_ref, bias_ref, alog_ref, skip_ref,
    gain_ref, ctx_out, mix_out,
    k_all, v_all, bias_scr, ctx_stage, mix_stage, gated, base_scr, er_scr, hs, runt, gmask,
    buf_a, buf_b, out_a, out_b, sloc_b, tot_b,
    k_send, k_recv, v_send, v_recv, a_send, a_recv, b_send, b_recv, o_send, o_recv,
):
    me = lax.axis_index("ctx")
    tok = q_ref.shape[0]
    half = tok // 2
    heads = dt_ref.shape[1]
    width = x_ref.shape[1]
    groups = b_ref.shape[1] // MN
    group_width = width // groups
    pieces, _, piece = buf_a.shape
    per_piece = piece // MP
    per_group = group_width // piece
    q_heads = q_ref.shape[1] // HEAD_SIZE
    repeat = q_ref.shape[1] // k_ref.shape[1]
    mesh_id = pl.DeviceIdType.MESH

    barrier = pltpu.get_barrier_semaphore()

    def greet(d, _):
        peer = lax.rem(me + d, n)
        pl.semaphore_signal(barrier, inc=1, device_id={"ctx": peer}, device_id_type=mesh_id)
        return 0

    lax.fori_loop(1, n, greet, 0)
    pl.semaphore_wait(barrier, n - 1)

    def remote(src, dst, send, recv, peer):
        return pltpu.make_async_remote_copy(
            src_ref=src, dst_ref=dst, send_sem=send, recv_sem=recv,
            device_id={"ctx": peer}, device_id_type=mesh_id,
        )

    def kv_copies(slot, sem_slot, peer, rows):
        return (
            remote(k_ref.at[rows], k_all.at[slot, rows], k_send.at[sem_slot], k_recv.at[slot], peer),
            remote(v_ref.at[rows], v_all.at[slot, rows], v_send.at[sem_slot], v_recv.at[slot], peer),
        )

    first = pl.ds(0, half)
    both = pl.ds(0, tok)

    def start_kv(d, _):
        @pl.when(me + d < n)
        def _():
            for copy in kv_copies(me, me + d, me + d, first):
                copy.start()

        @pl.when(me - d >= 0)
        def _():
            for copy in kv_copies(me, me - d, me - d, both):
                copy.start()

        return 0

    lax.fori_loop(1, n, start_kv, 0)

    raw = dt_ref[...].astype(F32) + bias_ref[...]
    steps = jnp.maximum(raw, 0.0) + jnp.log1p(jnp.exp(-jnp.abs(raw)))
    decay = -steps * jnp.exp(alog_ref[...])
    row = lax.broadcasted_iota(jnp.int32, (tok, tok), 0)
    col = lax.broadcasted_iota(jnp.int32, (tok, tok), 1)
    lower = (col <= row) & ((row < half) == (col < half))
    tri = lower.astype(F32)
    hs[0:tok, :] = dot(tri, decay, precision=HIGHEST)
    hs[tok : 2 * tok, :] = steps
    hs[2 * tok :, :] = jnp.broadcast_to(skip_ref[...], (8, heads))
    runt[...] = dot(decay, tri, 0, 1, precision=HIGHEST)
    for g in range(groups):
        cols = slice(g * MN, (g + 1) * MN)
        gmask[g] = jnp.where(lower, dot(c_ref[:, cols], b_ref[:, cols], 1, 1), 0.0)

    @pl.when(me == 0)
    def _():
        buf_a[...] = jnp.zeros_like(buf_a)

    lane_head = lax.broadcasted_iota(jnp.int32, (heads, piece), 1) // MP
    head_row = lax.broadcasted_iota(jnp.int32, (heads, piece), 0)
    wide_head = lax.broadcasted_iota(jnp.int32, (heads, per_piece * tok), 1) // tok
    wide_row = lax.broadcasted_iota(jnp.int32, (heads, per_piece * tok), 0)
    left = lax.broadcasted_iota(jnp.int32, (tok, 2 * MP), 1) < MP

    def place(src, dst_of, kind, block_id, which):
        owner = block_id // 2
        slot = lax.rem(block_id, 2)

        @pl.when(owner == me)
        def _():
            pltpu.make_async_copy(src, dst_of(slot), o_recv.at[kind, slot]).start()

        @pl.when(owner != me)
        def _():
            remote(src, dst_of(slot), o_send.at[kind, which], o_recv.at[kind, slot], owner).start()

    def block_id(which):
        return me if which == 0 else 2 * n - 1 - me

    def finish_group(k, which):
        @pl.when(lax.rem(k + 1, per_group) == 0)
        def _():
            g = k // per_group
            cols = pl.ds(pl.multiple_of(g * group_width, group_width), group_width)
            rows = pl.ds(which * half, half)
            value = gated[rows, cols].astype(F32)
            power = jnp.mean(value * value, axis=-1, keepdims=True)
            mix_stage[rows, cols] = (value * lax.rsqrt(power + NORM_EPS) * gain_ref[:, cols]).astype(BF16)
            place(
                mix_stage.at[rows, cols],
                lambda slot: mix_out.at[pl.ds(pl.multiple_of(slot * half, half), half), cols],
                g, block_id(which), which,
            )

    def silu(value):
        return value / (1.0 + jnp.exp(-value))

    def step_a(k):
        cols = pl.ds(pl.multiple_of(k * piece, piece), piece)
        g = k // per_group
        gcols = pl.ds(pl.multiple_of(g * MN, MN), MN)
        pick = (head_row == k * per_piece + lane_head).astype(F32)
        spread = dot(hs[...], pick, precision=HIGHEST)
        run, step, skip = spread[0:tok], spread[tok : 2 * tok], spread[2 * tok : 2 * tok + 1]
        xs = x_ref[:, cols].astype(F32)
        xdt = xs * step
        last_a, last_b = run[half - 1 : half], run[tok - 1 : tok]
        b_rows = b_ref[:, gcols]
        add_a = dot(b_rows[0:half], (xdt[0:half] * jnp.exp(last_a - run[0:half])).astype(BF16), 0, 0)
        sloc_b[k] = dot(b_rows[half:], (xdt[half:] * jnp.exp(last_b - run[half:])).astype(BF16), 0, 0)
        tot_b[k] = jnp.broadcast_to(jnp.exp(last_b), (8, piece))
        er = jnp.exp(run)
        er_scr[:, cols] = er[half:]

        @pl.when(me > 0)
        def _():
            remote(out_a.at[k], buf_a.at[k], a_send.at[k], a_recv.at[k], me).wait_recv()

        state = (buf_a[k].astype(F32) * jnp.exp(last_a) + add_a).astype(BF16)

        @pl.when(me < n - 1)
        def _():
            out_a[k] = state
            remote(out_a.at[k], buf_a.at[k], a_send.at[k], a_recv.at[k], me + 1).start()

        @pl.when(me == n - 1)
        def _():
            buf_b[k] = state

        wide = dot(hs[0:tok, :], (wide_row == k * per_piece + wide_head).astype(F32), precision=HIGHEST)
        gm = gmask[g]
        inner = []
        for pair in range(per_piece // 2):
            weights = []
            for which in range(2):
                h = 2 * pair + which
                gap = wide[:, h * tok : (h + 1) * tok] - runt[pl.ds(k * per_piece + h, 1), :]
                weights.append((jnp.exp(jnp.minimum(gap, 0.0)) * gm).astype(BF16))
            part = xdt[:, pair * 2 * MP : (pair + 1) * 2 * MP]
            stacked = jnp.concatenate(
                [jnp.where(left, part, 0.0).astype(BF16), jnp.where(left, 0.0, part).astype(BF16)], axis=0
            )
            inner.append(dot(jnp.concatenate(weights, axis=1), stacked))
        base = jnp.concatenate(inner, axis=1) + skip * xs
        base_scr[:, cols] = base[half:]
        carried = dot(c_ref[0:half, gcols], buf_a[k]) * er[0:half]
        z = z_ref[0:half, cols].astype(F32)
        gated[0:half, cols] = ((base[0:half] + carried) * silu(z)).astype(BF16)
        finish_group(k, 0)

    def step_b(k):
        cols = pl.ds(pl.multiple_of(k * piece, piece), piece)
        gcols = pl.ds(pl.multiple_of((k // per_group) * MN, MN), MN)

        @pl.when(me < n - 1)
        def _():
            remote(out_b.at[k], buf_b.at[k], b_send.at[k], b_recv.at[k], me).wait_recv()

        @pl.when(me > 0)
        def _():
            out_b[k] = (buf_b[k].astype(F32) * tot_b[k][0:1] + sloc_b[k]).astype(BF16)
            remote(out_b.at[k], buf_b.at[k], b_send.at[k], b_recv.at[k], me - 1).start()

        carried = dot(c_ref[half:, gcols], buf_b[k]) * er_scr[:, cols]
        z = z_ref[half:, cols].astype(F32)
        gated[half:, cols] = ((base_scr[:, cols] + carried) * silu(z)).astype(BF16)
        finish_group(k, 1)

    def attention():
        def wait_kv(s, _):
            @pl.when(s < me)
            def _():
                for copy in kv_copies(s, s, me, first):
                    copy.wait_recv()
                k_all[s, half:, :] = jnp.zeros((half, k_ref.shape[1]), BF16)
                v_all[s, half:, :] = jnp.zeros((half, k_ref.shape[1]), BF16)

            @pl.when(s > me)
            def _():
                for copy in kv_copies(s, s, me, both):
                    copy.wait_recv()

            return 0

        lax.fori_loop(0, n, wait_kv, 0)
        k_all[me] = k_ref[...]
        v_all[me] = v_ref[...]
        key = lax.broadcasted_iota(jnp.int32, (tok, n * tok), 1)
        source = key // tok
        within = key - source * tok
        key_pos = jnp.where(
            within < half, source * half + within, (2 * n - 2 - source) * half + within
        )
        query = lax.broadcasted_iota(jnp.int32, (tok, n * tok), 0)
        query_pos = jnp.where(query < half, me * half + query, (2 * n - 2 - me) * half + query)
        bias_scr[...] = jnp.where(key_pos <= query_pos, 0.0, MASKED)
        scale = 1.0 / math.sqrt(HEAD_SIZE)

        def one_head(h, _):
            hcols = pl.ds(pl.multiple_of(h * HEAD_SIZE, HEAD_SIZE), HEAD_SIZE)
            kcols = pl.ds(pl.multiple_of((h // repeat) * HEAD_SIZE, HEAD_SIZE), HEAD_SIZE)
            keys = k_all[:, :, kcols].reshape(n * tok, HEAD_SIZE)
            values = v_all[:, :, kcols].reshape(n * tok, HEAD_SIZE)
            scores = dot(q_ref[:, hcols], keys, 1, 1) * scale + bias_scr[...]
            expo = jnp.exp(scores - jnp.max(scores, axis=-1, keepdims=True))
            total = jnp.sum(expo, axis=-1, keepdims=True)
            ctx_stage[:, hcols] = (dot(expo.astype(BF16), values) / total).astype(BF16)
            return 0

        lax.fori_loop(0, q_heads, one_head, 0)
        for which in range(2):
            place(
                ctx_stage.at[pl.ds(which * half, half)],
                lambda slot: ctx_out.at[pl.ds(pl.multiple_of(slot * half, half), half)],
                groups, block_id(which), which,
            )

    lag = 2 * n - 1
    last = pieces + lag
    attend_at = jnp.where(me == 0, lag, last)

    def slot_step(t, _):
        k_a = t - me
        k_b = t - (lag - me)

        @pl.when((k_a >= 0) & (k_a < pieces))
        def _():
            step_a(k_a)

        @pl.when(t == attend_at)
        def _():
            attention()

        @pl.when((k_b >= 0) & (k_b < pieces))
        def _():
            step_b(k_b)

        return 0

    lax.fori_loop(0, last + 1, slot_step, 0)

    def drain(k, _):
        @pl.when(me < n - 1)
        def _():
            remote(out_a.at[k], buf_a.at[k], a_send.at[k], a_recv.at[k], me).wait_send()

        @pl.when(me > 0)
        def _():
            remote(out_b.at[k], buf_b.at[k], b_send.at[k], b_recv.at[k], me).wait_send()

        return 0

    lax.fori_loop(0, pieces, drain, 0)

    def drain_kv(s, _):
        @pl.when(s > me)
        def _():
            for copy in kv_copies(s, s, me, first):
                copy.wait_send()

        @pl.when(s < me)
        def _():
            for copy in kv_copies(s, s, me, both):
                copy.wait_send()

        return 0

    lax.fori_loop(0, n, drain_kv, 0)

    for which in range(2):
        rows = pl.ds(which * half, half)
        for kind in range(groups + 1):
            if kind < groups:
                cols = pl.ds(kind * group_width, group_width)
                src, dst = mix_stage.at[rows, cols], mix_out.at[rows, cols]
            else:
                src, dst = ctx_stage.at[rows], ctx_out.at[rows]
            copy = remote(src, dst, o_send.at[kind, which], o_recv.at[kind, which], me)

            @pl.when(block_id(which) // 2 != me)
            def _():
                copy.wait_send()

            copy.wait_recv()


def body(n, query, keys, values, m_x, m_z, m_b, m_c, dt_raw, dt_bias, a_log, d_skip, norm_gain):
    tok, width = m_x.shape
    half = tok // 2
    heads = dt_raw.shape[1]
    groups = m_b.shape[1] // MN
    piece = math.gcd(width // groups, 256)
    pieces = width // piece
    kv = keys.shape[1]
    dma = pltpu.SemaphoreType.DMA
    vmem = pltpu.VMEM
    state = (pieces, MN, piece)
    spec = pl.BlockSpec(memory_space=pltpu.VMEM)
    return pl.pallas_call(
        functools.partial(kernel, n),
        out_shape=(
            jax.ShapeDtypeStruct(query.shape, BF16),
            jax.ShapeDtypeStruct(m_x.shape, BF16),
        ),
        in_specs=[spec] * 12,
        out_specs=(spec, spec),
        scratch_shapes=[
            vmem((n, tok, kv), BF16),
            vmem((n, tok, kv), BF16),
            vmem((tok, n * tok), F32),
            vmem(query.shape, BF16),
            vmem(m_x.shape, BF16),
            vmem(m_x.shape, BF16),
            vmem((half, width), F32),
            vmem((half, width), F32),
            vmem((2 * tok + 8, heads), F32),
            vmem((heads, tok), F32),
            vmem((groups, tok, tok), F32),
            vmem(state, BF16),
            vmem(state, BF16),
            vmem(state, BF16),
            vmem(state, BF16),
            vmem(state, F32),
            vmem((pieces, 8, piece), F32),
            dma((n,)),
            dma((n,)),
            dma((n,)),
            dma((n,)),
            dma((pieces,)),
            dma((pieces,)),
            dma((pieces,)),
            dma((pieces,)),
            dma((groups + 1, 2)),
            dma((groups + 1, 2)),
        ],
        compiler_params=pltpu.CompilerParams(
            collective_id=0, has_side_effects=True, vmem_limit_bytes=48 * 1024 * 1024
        ),
    )(
        query, keys, values, m_x, m_z, m_b, m_c, dt_raw,
        dt_bias.reshape(1, -1), a_log.reshape(1, -1), d_skip.reshape(1, -1), norm_gain.reshape(1, -1),
    )


def solution(mesh):
    rows = P(("grp", "ctx"), "hd")
    in_specs = (rows,) * 8 + (P("hd"),) * 4
    return jax.shard_map(
        functools.partial(body, mesh.shape["ctx"]),
        mesh=mesh, in_specs=in_specs, out_specs=(rows, rows), check_vma=False,
    )
```

time: 160 us -> 72 us (0.45)
  blocking collectives: 71.8 us -> 0 us
  Pallas kernels: 0 us -> 62.1 us
  waiting for transfers between devices: 30.6 us -> 0 us
  starting transfers between devices: 20.3 us -> 0 us
  local copies, waits for them, and re-layouts: 20.3 us -> 8.73 us
  matrix products: 7.27 us -> 0 us
  other arithmetic: 7.03 us -> 0 us
    all_gather x5 -> x0, blocking collectives: 71.8 us -> none  [the longest x1 15.9 us: attend(): value_piece = lax.all_gather(values, 'ctx', axis=0, tiled=True)]
    pallas_call x0 -> x1, Pallas kernels: none -> 62.1 us  [body(): pl.pallas_call(functools.partial(kernel, n), out_shape=(jax.ShapeDtypeStr...]
    all_to_all x5 -> x0, waiting for transfers between devices: 30.6 us -> none  [the longest x1 11.7 us: body(): lax.all_to_all(m_x, 'ctx', split_axis=1, concat_axis=0, tiled=True)]
    all_to_all x5 -> x0, starting transfers between devices: 20.3 us -> none  [the longest x1 4.99 us: body(): lax.all_to_all(gated, 'ctx', split_axis=0, concat_axis=1, tiled=True)]
    dot_general x6 -> x0, matrix products: 7.27 us -> none  [the longest x1 2.7 us: ssd_block(): inner = jnp.einsum('ijh,jhp->ihp', weights, inputs, precision=highest)]
    unnamed x36 -> x25, local copies, waits for them, and re-layouts: 12 us -> 8.73 us
    reshape x5 -> x0, local copies, waits for them, and re-layouts: 2.37 us -> none  [the longest x1 1.12 us: attend(): query_heads = query.reshape(tok_rows, kv_local, heads_per_group, HEAD_SIZE)]
    all_to_all x4 -> x0, local copies, waits for them, and re-layouts: 1.81 us -> none  [the longest x1 1.12 us: body(): lax.all_to_all(context_cols, 'ctx', split_axis=0, concat_axis=1, tiled=True)]
  transfers between devices with their start and end apart: 5 -> 0, of which waited for: 3 -> 0; matrix products, arithmetic and copies ran while one was open for 17% -> 0% of each run, Pallas kernels for 0% -> 0%
where the time goes in v1:
time: 72 us; the launch traced here: 71.6 us
  Pallas kernels  62.1 us (86%)
  local copies, waits for them, and re-layouts  8.73 us (12%)
    pallas_call x1, Pallas kernels, body(): pl.pallas_call(functools.partial(kernel, n), out_shape=(jax.ShapeDtypeStr...  62.1 us
    unnamed x25, local copies, waits for them, and re-layouts  8.73 us

profile of v1, /device:TPU:0, one launch (start us, length us, event | category | flops | bytes accessed | tf_op | source)
XLA Modules:
  0.0 71.6 jit_solution(10432637340864920551)
XLA Ops:
  0.6 0.0 copy-start.7
  0.6 0.0 copy-start.8
  0.7 0.0 copy-start.9
  0.7 0.0 copy-start.10
  0.7 0.8 %copy.14.dt_ref = bf16[128,32]{1,0:T(8,128)(2,1)S(1)} copy(bf16[128,32]{0,1:T(8,128)(2,1)} %param.19) | data formatting | bytes 16384 | tf_op args[7]
  1.5 0.0 copy-done.7
  1.5 0.0 copy-done.8
  1.5 0.0 copy-done.9
  1.5 0.0 copy-done.10
  1.5 0.0 copy-start
  1.6 1.0 %copy-done = bf16[128,2048]{1,0:T(8,128)(2,1)S(1)} copy-done((bf16[128,2048]{1,0:T(8,128)(2,1)S(1)}, bf16[128,2048]{1,0:T(8,128)(2,1)}, u32[]{:S(2)}) %copy-start) | copy-done | bytes 524312
  2.6 0.0 copy-start.1
  2.6 1.0 %copy-done.1 = bf16[128,2048]{1,0:T(8,128)(2,1)S(1)} copy-done((bf16[128,2048]{1,0:T(8,128)(2,1)S(1)}, bf16[128,2048]{1,0:T(8,128)(2,1)}, u32[]{:S(2)}) %copy-start.1) | copy-done | bytes 524312
  3.6 0.0 copy-start.2
  3.6 0.9 %copy-done.2 = bf16[128,1024]{1,0:T(8,128)(2,1)S(1)} copy-done((bf16[128,1024]{1,0:T(8,128)(2,1)S(1)}, bf16[128,1024]{1,0:T(8,128)(2,1)}, u32[]{:S(2)}) %copy-start.2) | copy-done | bytes 262168
  4.6 0.0 copy-start.3
  4.6 0.8 %copy-done.3 = bf16[128,256]{1,0:T(8,128)(2,1)S(1)} copy-done((bf16[128,256]{1,0:T(8,128)(2,1)S(1)}, bf16[128,256]{1,0:T(8,128)(2,1)}, u32[]{:S(2)}) %copy-start.3) | copy-done | bytes 65560
  5.4 0.0 copy-start.4
  5.4 0.8 %copy-done.4 = bf16[128,256]{1,0:T(8,128)(2,1)S(1)} copy-done((bf16[128,256]{1,0:T(8,128)(2,1)S(1)}, bf16[128,256]{1,0:T(8,128)(2,1)}, u32[]{:S(2)}) %copy-start.4) | copy-done | bytes 65560
  6.3 0.0 copy-start.5
  6.3 0.8 %copy-done.5 = bf16[128,256]{1,0:T(8,128)(2,1)S(1)} copy-done((bf16[128,256]{1,0:T(8,128)(2,1)S(1)}, bf16[128,256]{1,0:T(8,128)(2,1)}, u32[]{:S(2)}) %copy-start.5) | copy-done | bytes 65560
  7.1 0.0 copy-start.6
  7.1 0.8 %copy-done.6 = bf16[128,256]{1,0:T(8,128)(2,1)S(1)} copy-done((bf16[128,256]{1,0:T(8,128)(2,1)S(1)}, bf16[128,256]{1,0:T(8,128)(2,1)}, u32[]{:S(2)}) %copy-start.6) | copy-done | bytes 65560
  7.9 62.1 %shard_map.131 = (bf16[128,1024]{1,0:T(8,128)(2,1)S(1)}, bf16[128,2048]{1,0:T(8,128)(2,1)S(1)}) custom-call(bf16[128,1024]{1,0:T(8,128)(2,1)S(1)} %copy-done.2, bf16[128,256]{1,0:T(8,128)(2,1)S(1)} %copy-done.3, bf16[128,256]{1,0:T(8,128)(2,1)S(1)} %copy-done.4, bf16[128,2048]{1,0:T(8,128)(2,1)S(1)} %copy-done, bf16[128,2048]{1,0:T(8,128)(2,1)S(1)} %copy-done.1, ...), custom_call_target="tpu_custom_call" | custom-call | tf_op jit(solution)/shard_map/pallas_call | solution.py:347
  70.1 0.7 copy.17
  70.8 0.8 %copy.18 = bf16[128,2048]{1,0:T(8,128)(2,1)} copy(bf16[128,2048]{1,0:T(8,128)(2,1)S(1)} %get-tuple-element.5) | data formatting | bytes 1048576
Async XLA Ops:
  0.6 0.9 %copy-start.7 = (f32[2048]{0:T(1024)S(1)}, f32[2048]{0:T(1024)}, u32[]{:S(2)}) copy-start(f32[2048]{0:T(1024)} %param.23) | copy-start | bytes 24580
  0.6 0.9 %copy-start.8 = (f32[32]{0:T(128)S(1)}, f32[32]{0:T(128)}, u32[]{:S(2)}) copy-start(f32[32]{0:T(128)} %param.20) | copy-start | bytes 388
  0.7 0.9 %copy-start.9 = (f32[32]{0:T(128)S(1)}, f32[32]{0:T(128)}, u32[]{:S(2)}) copy-start(f32[32]{0:T(128)} %param.21) | copy-start | bytes 388
  0.7 0.9 %copy-start.10 = (f32[32]{0:T(128)S(1)}, f32[32]{0:T(128)}, u32[]{:S(2)}) copy-start(f32[32]{0:T(128)} %param.22) | copy-start | bytes 388
  1.5 1.0 %copy-start = (bf16[128,2048]{1,0:T(8,128)(2,1)S(1)}, bf16[128,2048]{1,0:T(8,128)(2,1)}, u32[]{:S(2)}) copy-start(bf16[128,2048]{1,0:T(8,128)(2,1)} %x_ref.1) | copy-start | bytes 1572868
  2.6 1.0 %copy-start.1 = (bf16[128,2048]{1,0:T(8,128)(2,1)S(1)}, bf16[128,2048]{1,0:T(8,128)(2,1)}, u32[]{:S(2)}) copy-start(bf16[128,2048]{1,0:T(8,128)(2,1)} %z_ref.1) | copy-start | bytes 1572868
  3.6 0.9 %copy-start.2 = (bf16[128,1024]{1,0:T(8,128)(2,1)S(1)}, bf16[128,1024]{1,0:T(8,128)(2,1)}, u32[]{:S(2)}) copy-start(bf16[128,1024]{1,0:T(8,128)(2,1)} %q_ref.1) | copy-start | bytes 786436
  4.6 0.8 %copy-start.3 = (bf16[128,256]{1,0:T(8,128)(2,1)S(1)}, bf16[128,256]{1,0:T(8,128)(2,1)}, u32[]{:S(2)}) copy-start(bf16[128,256]{1,0:T(8,128)(2,1)} %k_ref.1) | copy-start | bytes 196612
  5.4 0.8 %copy-start.4 = (bf16[128,256]{1,0:T(8,128)(2,1)S(1)}, bf16[128,256]{1,0:T(8,128)(2,1)}, u32[]{:S(2)}) copy-start(bf16[128,256]{1,0:T(8,128)(2,1)} %v_ref.1) | copy-start | bytes 196612
  6.3 0.8 %copy-start.5 = (bf16[128,256]{1,0:T(8,128)(2,1)S(1)}, bf16[128,256]{1,0:T(8,128)(2,1)}, u32[]{:S(2)}) copy-start(bf16[128,256]{1,0:T(8,128)(2,1)} %b_ref.1) | copy-start | bytes 196612
  7.1 0.8 %copy-start.6 = (bf16[128,256]{1,0:T(8,128)(2,1)S(1)}, bf16[128,256]{1,0:T(8,128)(2,1)}, u32[]{:S(2)}) copy-start(bf16[128,256]{1,0:T(8,128)(2,1)} %c_ref.1) | copy-start | bytes 196612

commit v2 on v1

--- a/solution.py
+++ b/solution.py
@@ -16,6 +16,9 @@
 HIGHEST = lax.Precision.HIGHEST
 F32 = jnp.float32
 BF16 = jnp.bfloat16
+INPUT_SPACE = pltpu.HBM
+HOP_SLOTS = 3
+PIECE = 256
 
 
 def dot(a, b, ca=1, cb=0, precision=None):
@@ -25,16 +28,17 @@
 
 
 def kernel(
-    n, q_ref, k_ref, v_ref, x_ref, z_ref, b_ref, c_ref, dt_ref, bias_ref, alog_ref, skip_ref,
-    gain_ref, ctx_out, mix_out,
-    k_all, v_all, bias_scr, ctx_stage, mix_stage, gated, base_scr, er_scr, hs, runt, gmask,
-    buf_a, buf_b, out_a, out_b, sloc_b, tot_b,
-    k_send, k_recv, v_send, v_recv, a_send, a_recv, b_send, b_recv, o_send, o_recv,
+    n, q_in, k_ref, v_ref, x_in, z_in, b_in, c_in, dt_in, bias_in, alog_in, skip_in,
+    gain_in, ctx_out, mix_out,
+    q_ref, x_ref, z_ref, b_ref, c_ref, dt_ref, bias_ref, alog_ref, skip_ref, gain_ref,
+    k_all, v_all, bias_scr, ctx_stage, arrived, gated, base_scr, er_scr, xdt_scr, hs, runt, gmask,
+    buf_a, buf_b, out_a, out_b, sloc_a, sloc_b, tot_a, tot_b,
+    k_send, k_recv, v_send, v_recv, a_send, a_recv, b_send, b_recv, o_send, o_recv, load_sem,
 ):
     me = lax.axis_index("ctx")
     tok = q_ref.shape[0]
     half = tok // 2
-    heads = dt_ref.shape[1]
+    heads = dt_ref.shape[0]
     width = x_ref.shape[1]
     groups = b_ref.shape[1] // MN
     group_width = width // groups
@@ -45,6 +49,19 @@
     repeat = q_ref.shape[1] // k_ref.shape[1]
     mesh_id = pl.DeviceIdType.MESH
 
+    loads = [
+        pltpu.make_async_copy(src, dst, load_sem.at[i])
+        for i, (src, dst) in enumerate(
+            (
+                (dt_in, dt_ref), (bias_in, bias_ref), (alog_in, alog_ref), (skip_in, skip_ref),
+                (b_in, b_ref), (c_in, c_ref), (x_in, x_ref), (gain_in, gain_ref), (z_in, z_ref),
+                (k_ref, k_all.at[me]), (v_ref, v_all.at[me]), (q_in, q_ref),
+            )
+        )
+    ]
+    for load in loads:
+        load.start()
+
     barrier = pltpu.get_barrier_semaphore()
 
     def greet(d, _):
@@ -85,17 +102,21 @@
 
     lax.fori_loop(1, n, start_kv, 0)
 
-    raw = dt_ref[...].astype(F32) + bias_ref[...]
+    row = lax.broadcasted_iota(jnp.int32, (tok, tok), 0)
+    col = lax.broadcasted_iota(jnp.int32, (tok, tok), 1)
+    for load in loads[:4]:
+        load.wait()
+    raw = dot((row == col).astype(BF16), dt_ref[...], 1, 1) + bias_ref[...]
     steps = jnp.maximum(raw, 0.0) + jnp.log1p(jnp.exp(-jnp.abs(raw)))
     decay = -steps * jnp.exp(alog_ref[...])
-    row = lax.broadcasted_iota(jnp.int32, (tok, tok), 0)
-    col = lax.broadcasted_iota(jnp.int32, (tok, tok), 1)
     lower = (col <= row) & ((row < half) == (col < half))
     tri = lower.astype(F32)
     hs[0:tok, :] = dot(tri, decay, precision=HIGHEST)
     hs[tok : 2 * tok, :] = steps
     hs[2 * tok :, :] = jnp.broadcast_to(skip_ref[...], (8, heads))
     runt[...] = dot(decay, tri, 0, 1, precision=HIGHEST)
+    for load in loads[4:6]:
+        load.wait()
     for g in range(groups):
         cols = slice(g * MN, (g + 1) * MN)
         gmask[g] = jnp.where(lower, dot(c_ref[:, cols], b_ref[:, cols], 1, 1), 0.0)
@@ -125,28 +146,20 @@
     def block_id(which):
         return me if which == 0 else 2 * n - 1 - me
 
-    def finish_group(k, which):
-        @pl.when(lax.rem(k + 1, per_group) == 0)
-        def _():
-            g = k // per_group
-            cols = pl.ds(pl.multiple_of(g * group_width, group_width), group_width)
-            rows = pl.ds(which * half, half)
-            value = gated[rows, cols].astype(F32)
-            power = jnp.mean(value * value, axis=-1, keepdims=True)
-            mix_stage[rows, cols] = (value * lax.rsqrt(power + NORM_EPS) * gain_ref[:, cols]).astype(BF16)
-            place(
-                mix_stage.at[rows, cols],
-                lambda slot: mix_out.at[pl.ds(pl.multiple_of(slot * half, half), half), cols],
-                g, block_id(which), which,
-            )
+    def send_piece(k, which):
+        cols = pl.ds(pl.multiple_of(k * piece, piece), piece)
+        place(
+            gated.at[pl.ds(which * half, half), cols],
+            lambda slot: arrived.at[pl.ds(pl.multiple_of(slot * half, half), half), cols],
+            k, block_id(which), which,
+        )
 
     def silu(value):
         return value / (1.0 + jnp.exp(-value))
 
-    def step_a(k):
+    def prepare(k):
         cols = pl.ds(pl.multiple_of(k * piece, piece), piece)
-        g = k // per_group
-        gcols = pl.ds(pl.multiple_of(g * MN, MN), MN)
+        gcols = pl.ds(pl.multiple_of((k // per_group) * MN, MN), MN)
         pick = (head_row == k * per_piece + lane_head).astype(F32)
         spread = dot(hs[...], pick, precision=HIGHEST)
         run, step, skip = spread[0:tok], spread[tok : 2 * tok], spread[2 * tok : 2 * tok + 1]
@@ -154,29 +167,18 @@
         xdt = xs * step
         last_a, last_b = run[half - 1 : half], run[tok - 1 : tok]
         b_rows = b_ref[:, gcols]
-        add_a = dot(b_rows[0:half], (xdt[0:half] * jnp.exp(last_a - run[0:half])).astype(BF16), 0, 0)
+        sloc_a[k] = dot(b_rows[0:half], (xdt[0:half] * jnp.exp(last_a - run[0:half])).astype(BF16), 0, 0)
         sloc_b[k] = dot(b_rows[half:], (xdt[half:] * jnp.exp(last_b - run[half:])).astype(BF16), 0, 0)
+        tot_a[k] = jnp.broadcast_to(jnp.exp(last_a), (8, piece))
         tot_b[k] = jnp.broadcast_to(jnp.exp(last_b), (8, piece))
-        er = jnp.exp(run)
-        er_scr[:, cols] = er[half:]
-
-        @pl.when(me > 0)
-        def _():
-            remote(out_a.at[k], buf_a.at[k], a_send.at[k], a_recv.at[k], me).wait_recv()
-
-        state = (buf_a[k].astype(F32) * jnp.exp(last_a) + add_a).astype(BF16)
-
-        @pl.when(me < n - 1)
-        def _():
-            out_a[k] = state
-            remote(out_a.at[k], buf_a.at[k], a_send.at[k], a_recv.at[k], me + 1).start()
-
-        @pl.when(me == n - 1)
-        def _():
-            buf_b[k] = state
-
+        er_scr[:, cols] = jnp.exp(run)
+        xdt_scr[:, cols] = xdt.astype(BF16)
+        base_scr[:, cols] = skip * xs
+
+    def within_blocks(k, _):
+        cols = pl.ds(pl.multiple_of(k * piece, piece), piece)
         wide = dot(hs[0:tok, :], (wide_row == k * per_piece + wide_head).astype(F32), precision=HIGHEST)
-        gm = gmask[g]
+        gm = gmask[k // per_group]
         inner = []
         for pair in range(per_piece // 2):
             weights = []
@@ -184,22 +186,48 @@
                 h = 2 * pair + which
                 gap = wide[:, h * tok : (h + 1) * tok] - runt[pl.ds(k * per_piece + h, 1), :]
                 weights.append((jnp.exp(jnp.minimum(gap, 0.0)) * gm).astype(BF16))
-            part = xdt[:, pair * 2 * MP : (pair + 1) * 2 * MP]
-            stacked = jnp.concatenate(
-                [jnp.where(left, part, 0.0).astype(BF16), jnp.where(left, 0.0, part).astype(BF16)], axis=0
-            )
+            at = pl.ds(pl.multiple_of(k * piece + pair * 2 * MP, 2 * MP), 2 * MP)
+            part = xdt_scr[:, at]
+            none = jnp.zeros_like(part)
+            stacked = jnp.concatenate([jnp.where(left, part, none), jnp.where(left, none, part)], axis=0)
             inner.append(dot(jnp.concatenate(weights, axis=1), stacked))
-        base = jnp.concatenate(inner, axis=1) + skip * xs
-        base_scr[:, cols] = base[half:]
-        carried = dot(c_ref[0:half, gcols], buf_a[k]) * er[0:half]
-        z = z_ref[0:half, cols].astype(F32)
-        gated[0:half, cols] = ((base[0:half] + carried) * silu(z)).astype(BF16)
-        finish_group(k, 0)
-
-    def step_b(k):
+        base_scr[:, cols] = base_scr[:, cols] + jnp.concatenate(inner, axis=1)
+        return 0
+
+    def gate(k, which, buffer):
         cols = pl.ds(pl.multiple_of(k * piece, piece), piece)
         gcols = pl.ds(pl.multiple_of((k // per_group) * MN, MN), MN)
-
+        rows = slice(which * half, (which + 1) * half)
+        carried = dot(c_ref[rows, gcols], buffer[k]) * er_scr[rows, cols]
+        z = z_ref[rows, cols].astype(F32)
+        gated[rows, cols] = ((base_scr[rows, cols] + carried) * silu(z)).astype(BF16)
+        send_piece(k, which)
+
+    def gate_a(k, _):
+        gate(k, 0, buf_a)
+        return 0
+
+    def step_a(k):
+        @pl.when(me == 0)
+        def _():
+            prepare(k)
+
+        @pl.when(me > 0)
+        def _():
+            remote(out_a.at[k], buf_a.at[k], a_send.at[k], a_recv.at[k], me).wait_recv()
+
+        state = (buf_a[k].astype(F32) * tot_a[k][0:1] + sloc_a[k]).astype(BF16)
+
+        @pl.when(me < n - 1)
+        def _():
+            out_a[k] = state
+            remote(out_a.at[k], buf_a.at[k], a_send.at[k], a_recv.at[k], me + 1).start()
+
+        @pl.when(me == n - 1)
+        def _():
+            buf_b[k] = state
+
+    def step_b(k):
         @pl.when(me < n - 1)
         def _():
             remote(out_b.at[k], buf_b.at[k], b_send.at[k], b_recv.at[k], me).wait_recv()
@@ -209,10 +237,7 @@
             out_b[k] = (buf_b[k].astype(F32) * tot_b[k][0:1] + sloc_b[k]).astype(BF16)
             remote(out_b.at[k], buf_b.at[k], b_send.at[k], b_recv.at[k], me - 1).start()
 
-        carried = dot(c_ref[half:, gcols], buf_b[k]) * er_scr[:, cols]
-        z = z_ref[half:, cols].astype(F32)
-        gated[half:, cols] = ((base_scr[:, cols] + carried) * silu(z)).astype(BF16)
-        finish_group(k, 1)
+        gate(k, 1, buf_b)
 
     def attention():
         def wait_kv(s, _):
@@ -231,8 +256,8 @@
             return 0
 
         lax.fori_loop(0, n, wait_kv, 0)
-        k_all[me] = k_ref[...]
-        v_all[me] = v_ref[...]
+        for load in loads[9:]:
+            load.wait()
         key = lax.broadcasted_iota(jnp.int32, (tok, n * tok), 1)
         source = key // tok
         within = key - source * tok
@@ -260,16 +285,34 @@
             place(
                 ctx_stage.at[pl.ds(which * half, half)],
                 lambda slot: ctx_out.at[pl.ds(pl.multiple_of(slot * half, half), half)],
-                groups, block_id(which), which,
+                pieces, block_id(which), which,
             )
 
-    lag = 2 * n - 1
+    for load in loads[6:9]:
+        load.wait()
+    lag = 2 * (n - 1) * HOP_SLOTS
     last = pieces + lag
-    attend_at = jnp.where(me == 0, lag, last)
+    b_start = lag - me * HOP_SLOTS
+    idle_between = me * HOP_SLOTS + pieces <= b_start
+    attend_at = jnp.where(idle_between, b_start, last)
+
+    def prepare_early(k, _):
+        prepare(k)
+        return 0
+
+    @pl.when(me > 0)
+    def _():
+        lax.fori_loop(0, pieces, prepare_early, 0)
+
+    inner_at = jnp.where(idle_between, b_start, 0)
 
     def slot_step(t, _):
-        k_a = t - me
-        k_b = t - (lag - me)
+        k_a = t - me * HOP_SLOTS
+        k_b = t - (lag - me * HOP_SLOTS)
+
+        @pl.when(t == inner_at)
+        def _():
+            lax.fori_loop(0, pieces, within_blocks, 0)
 
         @pl.when((k_a >= 0) & (k_a < pieces))
         def _():
@@ -278,6 +321,7 @@
         @pl.when(t == attend_at)
         def _():
             attention()
+            lax.fori_loop(0, pieces, gate_a, 0)
 
         @pl.when((k_b >= 0) & (k_b < pieces))
         def _():
@@ -315,29 +359,37 @@
 
     lax.fori_loop(0, n, drain_kv, 0)
 
+    def await_placed(kind, which, src, dst):
+        copy = remote(src, dst, o_send.at[kind, which], o_recv.at[kind, which], me)
+
+        @pl.when(block_id(which) // 2 != me)
+        def _():
+            copy.wait_send()
+
+        copy.wait_recv()
+
     for which in range(2):
         rows = pl.ds(which * half, half)
-        for kind in range(groups + 1):
-            if kind < groups:
-                cols = pl.ds(kind * group_width, group_width)
-                src, dst = mix_stage.at[rows, cols], mix_out.at[rows, cols]
-            else:
-                src, dst = ctx_stage.at[rows], ctx_out.at[rows]
-            copy = remote(src, dst, o_send.at[kind, which], o_recv.at[kind, which], me)
-
-            @pl.when(block_id(which) // 2 != me)
-            def _():
-                copy.wait_send()
-
-            copy.wait_recv()
+        await_placed(pieces, which, ctx_stage.at[rows], ctx_out.at[rows])
+    for g in range(groups):
+        gcols = slice(g * group_width, (g + 1) * group_width)
+        for which in range(2):
+            rows = pl.ds(which * half, half)
+            for k in range(g * per_group, (g + 1) * per_group):
+                cols = pl.ds(k * piece, piece)
+                await_placed(k, which, gated.at[rows, cols], arrived.at[rows, cols])
+            value = arrived[rows, gcols].astype(F32)
+            power = jnp.mean(value * value, axis=-1, keepdims=True)
+            mix_out[rows, gcols] = (value * lax.rsqrt(power + NORM_EPS) * gain_ref[:, gcols]).astype(BF16)
 
 
 def body(n, query, keys, values, m_x, m_z, m_b, m_c, dt_raw, dt_bias, a_log, d_skip, norm_gain):
     tok, width = m_x.shape
     half = tok // 2
     heads = dt_raw.shape[1]
+    anywhere = pl.BlockSpec(memory_space=INPUT_SPACE)
     groups = m_b.shape[1] // MN
-    piece = math.gcd(width // groups, 256)
+    piece = math.gcd(width // groups, PIECE)
     pieces = width // piece
     kv = keys.shape[1]
     dma = pltpu.SemaphoreType.DMA
@@ -350,17 +402,28 @@
             jax.ShapeDtypeStruct(query.shape, BF16),
             jax.ShapeDtypeStruct(m_x.shape, BF16),
         ),
-        in_specs=[spec] * 12,
+        in_specs=[anywhere] * 12,
         out_specs=(spec, spec),
         scratch_shapes=[
+            vmem(query.shape, BF16),
+            vmem(m_x.shape, BF16),
+            vmem(m_x.shape, BF16),
+            vmem(m_b.shape, BF16),
+            vmem(m_b.shape, BF16),
+            vmem((heads, tok), BF16),
+            vmem((1, heads), F32),
+            vmem((1, heads), F32),
+            vmem((1, heads), F32),
+            vmem((1, width), F32),
             vmem((n, tok, kv), BF16),
             vmem((n, tok, kv), BF16),
             vmem((tok, n * tok), F32),
             vmem(query.shape, BF16),
             vmem(m_x.shape, BF16),
             vmem(m_x.shape, BF16),
-            vmem((half, width), F32),
-            vmem((half, width), F32),
+            vmem((tok, width), F32),
+            vmem((tok, width), F32),
+            vmem((tok, width), BF16),
             vmem((2 * tok + 8, heads), F32),
             vmem((heads, tok), F32),
             vmem((groups, tok, tok), F32),
@@ -369,6 +432,8 @@
             vmem(state, BF16),
             vmem(state, BF16),
             vmem(state, F32),
+            vmem(state, F32),
+            vmem((pieces, 8, piece), F32),
             vmem((pieces, 8, piece), F32),
             dma((n,)),
             dma((n,)),
@@ -378,14 +443,15 @@
             dma((pieces,)),
             dma((pieces,)),
             dma((pieces,)),
-            dma((groups + 1, 2)),
-            dma((groups + 1, 2)),
+            dma((pieces + 1, 2)),
+            dma((pieces + 1, 2)),
+            dma((12,)),
         ],
         compiler_params=pltpu.CompilerParams(
-            collective_id=0, has_side_effects=True, vmem_limit_bytes=48 * 1024 * 1024
+            collective_id=0, has_side_effects=True, vmem_limit_bytes=67043328
         ),
     )(
-        query, keys, values, m_x, m_z, m_b, m_c, dt_raw,
+        query, keys, values, m_x, m_z, m_b, m_c, dt_raw.T,
         dt_bias.reshape(1, -1), a_log.reshape(1, -1), d_skip.reshape(1, -1), norm_gain.reshape(1, -1),
     )
 

time: 72 us -> 61.5 us (0.85)
  local copies, waits for them, and re-layouts: 8.73 us -> 2.52 us
  Pallas kernels: 62.1 us -> 58.2 us
    unnamed x25 -> x4, local copies, waits for them, and re-layouts: 8.73 us -> 2.52 us
    pallas_call x1, Pallas kernels: 62.1 us -> 58.2 us  [body(): pl.pallas_call(functools.partial(kernel, n), out_shape=(jax.ShapeDtypeStr...]
where the time goes in v2:
time: 61.5 us; the launch traced here: 61.4 us
  Pallas kernels  58.2 us (95%)
  local copies, waits for them, and re-layouts  2.52 us (4%)
  between operations  0.65 us (1%)
    pallas_call x1, Pallas kernels, body(): pl.pallas_call(functools.partial(kernel, n), out_shape=(jax.ShapeDtypeStr...  58.2 us
    unnamed x4, local copies, waits for them, and re-layouts  2.52 us

profile of v2, /device:TPU:0, one launch (start us, length us, event | category | flops | bytes accessed | tf_op | source)
XLA Modules:
  0.0 61.4 jit_solution(9378831221821373060)
XLA Ops:
  0.6 58.2 %shard_map.131 = (bf16[128,1024]{1,0:T(8,128)(2,1)}, bf16[128,2048]{1,0:T(8,128)(2,1)}) custom-call(bf16[128,1024]{1,0:T(8,128)(2,1)} %q_in.1, bf16[128,256]{1,0:T(8,128)(2,1)} %k_ref.1, bf16[128,256]{1,0:T(8,128)(2,1)} %v_ref.1, bf16[128,2048]{1,0:T(8,128)(2,1)} %x_in.1, bf16[128,2048]{1,0:T(8,128)(2,1)} %z_in.1, bf16[128,256]{1,0:T(8,128)(2,1)} %b_in.1, ...), custom_call_target="tpu_custom_call" | custom-call | tf_op jit(solution)/shard_map/pallas_call | solution.py:399
  58.8 0.0 copy-start
  58.9 1.7 %copy.16 = bf16[128,1024]{1,0:T(8,128)(2,1)} copy(bf16[128,1024]{1,0:T(8,128)(2,1)} %get-tuple-element.4) | data formatting | bytes 524288
  60.6 0.0 copy-done
  60.6 0.8 %copy.17 = bf16[128,2048]{1,0:T(8,128)(2,1)} copy(bf16[128,2048]{1,0:T(8,128)(2,1)S(1)} %copy-done) | data formatting | bytes 1048576
Async XLA Ops:
  58.8 1.7 %copy-start = (bf16[128,2048]{1,0:T(8,128)(2,1)S(1)}, bf16[128,2048]{1,0:T(8,128)(2,1)}, u32[]{:S(2)}) copy-start(bf16[128,2048]{1,0:T(8,128)(2,1)} %get-tuple-element.5) | copy-start | bytes 1572868
